TPU v7x, 256 devices: a whole 4x4x8 slice. The times are simulated.
256 devices in a mesh: dp: 64 (over z, y, core), mp: 4 (over x).
Axes of the slice: x: 4, y: 4, z: 8, core: 2. Of those that a mesh axis runs over, the one named last changes fastest.
Arguments:
- latents: bfloat16 [2097152, 256], P(('dp', 'mp')), may hold values from -6 to 6
- proj_weight: bfloat16 [18, 256], replicated, may hold values from -0.375 to 0.375
- proj_bias: float32 [18], replicated, may hold values from -2.5 to 2.5
- fill: int32 [16384], replicated, may hold values from 0 to 128, as said below
- target: int32 [16384], replicated, may hold values from -1 to 63, as said below
- target_slot: int32 [16384], replicated, may hold values from -1 to 31, as said below
Outputs:
- latent_grad: bfloat16 [1048576, 256], P(('dp', 'mp'))
- weight_grad: float32 [18, 256], replicated
- entropy_loss: float32 [], replicated
Inputs may be any that keep to these rules, and one draw needn't show every extreme that they name: `fill`: zero exactly on the empty slots of a device, which are those whose target is -1. `target`: blocks go to devices with the same mp index. Each device receives exactly 32 blocks, one in each of its positions; at most 1 block goes from one device to any one index of dp, and some device does send 1 block to an index. -1 marks an empty slot. `target_slot`: -1 exactly where target is -1.
All inputs are finite; a program needn't handle non-finite values.
Results may differ from a plain program's by a relative error of at most 0.0049.
Values may be sent and summed in bfloat16 or wider, within the bound.
No kernel may reach another device: no remote copies, remote signals or barrier semaphores. Data moves between devices by JAX's collectives and lax.ppermute only.
A program may use at most 64 MiB of HBM per device.

v0:
```python
import functools

import jax
import jax.numpy as jnp
from jax import lax
from jax.sharding import Mesh
from jax.sharding import PartitionSpec as P

BLK = 128
OUT_SLOTS = 32
DP = ("dp_0", "dp_1", "dp_2")
DP_MP = ("dp_0", "dp_1", "dp_2", "mp")


sharpness = 2.0


def one_axis_at_a_time(x, axes):
    return functools.reduce(lax.psum, axes, x)


def routing(fill, target, target_slot, n_dp, n_mp, in_slots, capacity, own_dp, own_mp):
    col_shape = (n_dp, n_mp, in_slots)
    col_fill = lax.dynamic_index_in_dim(fill.reshape(col_shape), own_mp, 1, keepdims=False)
    col_target = lax.dynamic_index_in_dim(target.reshape(col_shape), own_mp, 1, keepdims=False)
    col_slot = lax.dynamic_index_in_dim(target_slot.reshape(col_shape), own_mp, 1, keepdims=False)
    matches = col_target[:, :, None] == col_target[:, None, :]
    earlier = lax.broadcasted_iota(jnp.int32, (in_slots, in_slots), 0) < lax.broadcasted_iota(
        jnp.int32, (in_slots, in_slots), 1
    )
    arrival_rank = jnp.sum((matches & earlier[None]).astype(jnp.int32), axis=1)
    sources = lax.broadcasted_iota(jnp.int32, (n_dp, in_slots), 0)
    arrive = sources * capacity + arrival_rank
    own_target = lax.dynamic_index_in_dim(col_target, own_dp, 0, keepdims=False)
    own_rank = lax.dynamic_index_in_dim(arrival_rank, own_dp, 0, keepdims=False)
    send_slot = jnp.where(own_target >= 0, own_target * capacity + own_rank, n_dp * capacity)
    chosen = (
        jnp.full((n_dp * capacity,), in_slots, jnp.int32)
        .at[send_slot]
        .set(jnp.arange(in_slots, dtype=jnp.int32), mode="drop")
    )
    landing = jnp.where(col_target == own_dp, col_slot, OUT_SLOTS).reshape(-1)
    gather_order = (
        jnp.zeros((OUT_SLOTS,), jnp.int32).at[landing].set(arrive.reshape(-1), mode="drop")
    )
    out_fill = jnp.zeros((OUT_SLOTS,), jnp.int32).at[landing].set(col_fill.reshape(-1), mode="drop")
    own_fill = lax.dynamic_index_in_dim(col_fill, own_dp, 0, keepdims=False)
    return (chosen, gather_order, out_fill, own_fill)


def statistics(blocks, fills, proj_weight, proj_bias):
    logits = (
        jnp.einsum("nkd,bd->nbk", blocks, proj_weight, preferred_element_type=jnp.float32)
        + proj_bias[None, :, None]
    )
    scaled = sharpness * logits
    token_mask = (lax.broadcasted_iota(jnp.int32, (1, 1, BLK), 2) < fills[:, None, None]).astype(
        jnp.float32
    )
    probability = jax.nn.sigmoid(scaled)
    entropy = jax.nn.softplus(scaled) - probability * scaled
    bit_sums = jnp.sum(probability * token_mask, axis=(0, 2))
    entropy_sum = jnp.sum(entropy * token_mask)
    variance = probability * (1.0 - probability) * token_mask
    return (bit_sums, entropy_sum, -2.0 * scaled * variance, 2.0 * variance)


def local(latents, proj_weight, proj_bias, fill, target, target_slot):
    n_dp = lax.axis_size(DP)
    n_mp = lax.axis_size("mp")
    own_dp = lax.axis_index(DP)
    own_mp = lax.axis_index("mp")
    feature_width = latents.shape[1]
    in_slots = latents.shape[0] // BLK
    capacity = max(1, 2 * OUT_SLOTS // n_dp)
    chosen, gather_order, out_fill, own_fill = routing(
        fill, target, target_slot, n_dp, n_mp, in_slots, capacity, own_dp, own_mp
    )
    token_count = jnp.sum(fill).astype(jnp.float32)
    loaded = latents.reshape(in_slots, BLK, feature_width)
    bit_sums, entropy_sum, first_term, second_term = statistics(
        loaded, own_fill, proj_weight, proj_bias
    )
    first_rounded = first_term.astype(jnp.bfloat16)
    second_rounded = second_term.astype(jnp.bfloat16)
    first_weight = jnp.einsum(
        "nbk,nkd->bd", first_rounded, loaded, preferred_element_type=jnp.float32
    )
    second_weight = jnp.einsum(
        "nbk,nkd->bd", second_rounded, loaded, preferred_element_type=jnp.float32
    )
    bit_sums, entropy_sum, first_weight, second_weight = (
        one_axis_at_a_time(bit_sums, DP_MP),
        one_axis_at_a_time(entropy_sum, DP_MP),
        one_axis_at_a_time(first_weight, DP_MP),
        one_axis_at_a_time(second_weight, DP_MP),
    )
    marginal = bit_sums / token_count
    codebook = -jnp.sum(marginal * jnp.log(marginal) + (1.0 - marginal) * jnp.log(1.0 - marginal))
    entropy_loss = entropy_sum / token_count - codebook
    log_odds = jnp.log(1.0 - marginal) - jnp.log(marginal)
    cotangent = (first_term - second_term * log_odds[None, :, None]).astype(jnp.bfloat16)
    padded_cot = jnp.concatenate(
        [cotangent, jnp.zeros((1,) + cotangent.shape[1:], cotangent.dtype)]
    )
    outgoing_cot = padded_cot[chosen].reshape(n_dp * capacity * cotangent.shape[1], BLK)
    arrived_cot = lax.all_to_all(outgoing_cot, DP, split_axis=0, concat_axis=0, tiled=True)
    landed = arrived_cot.reshape(n_dp * capacity, cotangent.shape[1], BLK)[gather_order]
    latent_grad = jnp.einsum(
        "nbk,bd->nkd", landed, proj_weight, preferred_element_type=jnp.float32
    ).astype(jnp.bfloat16)
    weight_grad = (first_weight - second_weight * log_odds[:, None]) / jnp.sqrt(token_count)
    return (latent_grad.reshape(-1, feature_width), weight_grad, entropy_loss)


def solution(mesh):
    torus = Mesh(mesh.devices.reshape(8, 4, 2, mesh.shape["mp"]), ("dp_0", "dp_1", "dp_2", "mp"))
    in_specs = (P(DP_MP, None), P(), P(), P(), P(), P())
    out_specs = (P(DP_MP, None), P(), P())
    return jax.shard_map(local, mesh=torus, in_specs=in_specs, out_specs=out_specs, check_vma=False)
```

profile of v0, /device:TPU:1, one launch (start us, length us, event | category | flops | bytes accessed | tf_op | source)
XLA Modules:
  0.0 117.3 jit_solution(832619779546663720)
XLA Ops:
  0.6 0.0 copy-start
  0.7 1.0 reshape.149
  1.6 1.5 %reduce_sum.46 = s32[]{:T(128)} reduce(s32[16384]{0:T(1024)} %param.9, s32[]{:T(128)} %constant.84.clone.1), dimensions={0}, to_apply=%region_5.6 | reduce | flops 16383 | bytes 65544 | tf_op jit(solution)/shard_map/reduce_sum | solution.py:79
  3.1 0.1 fusion.20
  3.2 0.0 copy-done
  3.2 0.0 copy-start.3
  3.2 4.2 %fusion.3 = (f32[]{:T(128)}, f32[18]{0:T(128)S(1)}, f32[18,64,128]{2,0,1:T(8,128)S(1)}) fusion(f32[64,128]{1,0:T(8,128)S(1)} %fusion.20, f32[18]{0:T(128)} %param.8, bf16[64,128,256]{2,1,0:T(8,128)(2,1)} %bitcast.87, bf16[18,256]{1,0:T(8,128)(2,1)S(1)} %copy-done), kind=kOutput, calls=%fused_computation.14 | convolution fusion | flops 78004208 | bytes 4826260 | tf_op jit(solution)/shard_map/nkd,bd->nbk/dot_general | solution.py:53
  7.4 0.0 copy-done.3
  7.4 0.8 convolution_bitcast_fusion.1
  8.2 0.0 copy-start.1
  8.2 0.0 copy-start.2
  8.2 0.8 convolution_bitcast_fusion
  9.7 0.0 copy-done.1
  9.7 0.1 reshape.150
  9.8 0.0 copy-done.2
  9.8 0.1 reshape.151
  9.9 0.1 fusion.19
  10.1 0.7 convert_reduce_fusion
  10.8 0.8 scatter_custom_fusion
  11.6 27.0 %all-reduce.1 = (f32[18]{0:T(128)S(1)}, f32[18,256]{1,0:T(8,128)S(1)}, f32[18,256]{1,0:T(8,128)S(1)}, f32[]{:T(128)}) all-reduce(f32[18]{0:T(128)S(1)} %get-tuple-element.4, f32[18,256]{1,0:T(8,128)S(1)} %convolution_bitcast_fusion.1, ...), channel_id=1, replica_groups=mesh['dp_0'=8,'dp_1'=4,'dp_2'=2,'mp'=4] {'dp_0'}, use_global_device_ids=true, to_apply=%region_1.2 | all-reduce | flops 9235 | bytes 73880 | tf_op jit(solution)/shard_map/psum | solution.py:19
  38.7 15.0 %all-reduce.3 = (f32[18]{0:T(128)S(1)}, f32[18,256]{1,0:T(8,128)S(1)}, f32[18,256]{1,0:T(8,128)S(1)}, f32[]{:T(128)}) all-reduce(f32[18]{0:T(128)S(1)} %get-tuple-element.5, f32[18,256]{1,0:T(8,128)S(1)} %get-tuple-element.6, f32[18,256]{1,0:T(8,128)S(1)} %get-tuple-element.7, ...), channel_id=1, replica_groups=mesh['dp_0'=8,'dp_1'=4,'dp_2'=2,'mp'=4] {'dp_1'}, use_global_device_ids=true, to_apply=%region_2.3 | all-reduce | flops 9235 | bytes 73880 | tf_op jit(solution)/shard_map/psum | solution.py:19
  53.7 15.9 %all-reduce.4 = (f32[18]{0:T(128)S(1)}, f32[18,256]{1,0:T(8,128)S(1)}, f32[18,256]{1,0:T(8,128)S(1)}, f32[]{:T(128)}) all-reduce(f32[18]{0:T(128)S(1)} %get-tuple-element.13, f32[18,256]{1,0:T(8,128)S(1)} %get-tuple-element.14, f32[18,256]{1,0:T(8,128)S(1)} %get-tuple-element.15, ...), channel_id=1, replica_groups=mesh['dp_0'=8,'dp_1'=4,'dp_2'=2,'mp'=4] {'dp_2'}, use_global_device_ids=true, to_apply=%region_3.4 | all-reduce | flops 9235 | bytes 73880 | tf_op jit(solution)/shard_map/psum | solution.py:19
  69.6 14.7 %all-reduce.2 = (f32[18]{0:T(128)S(1)}, f32[18,256]{1,0:T(8,128)S(1)}, f32[18,256]{1,0:T(8,128)S(1)}, f32[]{:T(128)}) all-reduce(f32[18]{0:T(128)S(1)} %get-tuple-element.17, f32[18,256]{1,0:T(8,128)S(1)} %get-tuple-element.18, f32[18,256]{1,0:T(8,128)S(1)} %get-tuple-element.19, ...), channel_id=1, replica_groups=mesh['dp_0'=8,'dp_1'=4,'dp_2'=2,'mp'=4] {'mp'}, use_global_device_ids=true, to_apply=%region_4.5 | all-reduce | flops 9235 | bytes 73880 | tf_op jit(solution)/shard_map/psum | solution.py:19
  84.3 0.6 fusion.29
  84.9 0.3 subtract_convert_fusion
  85.3 1.4 %gather_fusion = bf16[64,18,128]{2,1,0:T(8,128)(2,1)} fusion(bf16[65,18,128]{2,1,0:T(8,128)(2,1)S(1)} %concatenate.3, s32[1024]{0:T(1024)S(1)} %pad_clamp_fusion.1), kind=kCustom, calls=%fused_computation | custom fusion | bytes 590080 | tf_op jit(solution)/shard_map/gather | solution.py:106
  86.7 9.0 %all-to-all-start = ((bf16[64,18,128]{2,1,0:T(8,128)(2,1)}), bf16[64,18,128]{2,1,0:T(8,128)(2,1)S(1)}, u32[]{:S(2)}, u32[]{:S(2)}) async-start(bf16[64,18,128]{2,1,0:T(8,128)(2,1)} %gather_fusion), calls=%async_computation | async-start | bytes 786432 | tf_op jit(solution)/shard_map/all_to_all | solution.py:107
  95.7 0.1 select_n.80
  95.9 0.1 reshape.181
  97.3 15.5 %scatter_custom_fusion.1 = s32[32]{0:T(128)S(1)} fusion(s32[4096]{0:T(1024)S(1)} %bitcast.86, s32[4096]{0:T(1024)S(1)} %reshape.181, s32[]{:T(128)} %constant.84.clone.1), kind=kCustom, calls=%fused_computation.67 | custom fusion | bytes 132 | tf_op jit(solution)/shard_map/scatter | solution.py:44
  112.8 0.7 subtract_divide_fusion
  113.5 0.0 all-to-all-done
  113.5 0.6 gather_fusion.1
  114.1 2.1 %convolution_convert_fusion = bf16[32,128,256]{2,1,0:T(8,128)(2,1)} fusion(bf16[32,18,128]{2,1,0:T(8,128)(2,1)S(1)} %gather_fusion.1, bf16[18,256]{1,0:T(8,128)(2,1)S(1)} %copy-done), kind=kOutput, calls=%fused_computation.6 | convolution fusion | flops 38797312 | bytes 2253824 | tf_op jit(solution)/shard_map/nbk,bd->nkd/dot_general | solution.py:109
  (12 shorter events, 0.1 us)
Async XLA Ops:
  0.6 2.6 %copy-start = (bf16[18,256]{1,0:T(8,128)(2,1)S(1)}, bf16[18,256]{1,0:T(8,128)(2,1)}, u32[]{:S(2)}) copy-start(bf16[18,256]{1,0:T(8,128)(2,1)} %param.7) | copy-start | bytes 27652
  3.2 4.2 %copy-start.3 = (bf16[8192,256]{1,0:T(8,128)(2,1)S(1)}, bf16[8192,256]{1,0:T(8,128)(2,1)}, u32[]{:S(2)}) copy-start(bf16[8192,256]{1,0:T(8,128)(2,1)} %param.6) | copy-start | bytes 12582916
  8.2 1.4 %copy-start.1 = (s32[16384]{0:T(1024)S(1)}, s32[16384]{0:T(1024)}, u32[]{:S(2)}) copy-start(s32[16384]{0:T(1024)} %param.10) | copy-start | bytes 196612
  8.2 1.6 %copy-start.2 = (s32[16384]{0:T(1024)S(1)}, s32[16384]{0:T(1024)}, u32[]{:S(2)}) copy-start(s32[16384]{0:T(1024)} %param.11) | copy-start | bytes 196612
  86.7 26.8 %all-to-all-start = ((bf16[64,18,128]{2,1,0:T(8,128)(2,1)}), bf16[64,18,128]{2,1,0:T(8,128)(2,1)S(1)}, u32[]{:S(2)}, u32[]{:S(2)}) async-start(bf16[64,18,128]{2,1,0:T(8,128)(2,1)} %gather_fusion), calls=%async_computation | async-start | bytes 786432 | tf_op jit(solution)/shard_map/all_to_all | solution.py:107
where the time goes:
time: 118 us; the launch traced here: 117 us
  blocking collectives  72.6 us (62%)
  local copies, waits for them, and re-layouts  19.7 us (17%)
  starting transfers between devices  9.05 us (8%)
  matrix products  7.86 us (7%)
  other arithmetic  4.15 us (4%)
  between operations  3.98 us (3%)
    psum x4, blocking collectives, one_axis_at_a_time(): return functools.reduce(lax.psum, axes, x)  72.6 us
    scatter x1, local copies, waits for them, and re-layouts, routing(): jnp.zeros((OUT_SLOTS,), jnp.int32).at[landing]  15.5 us
    all_to_all x1, starting transfers between devices, local(): lax.all_to_all(outgoing_cot, DP, split_axis=0, concat_axis=0, tiled=True)  9.05 us
    dot_general x1, matrix products, statistics(): jnp.einsum('nkd,bd->nbk', blocks, proj_weight, preferred_element_type=jnp...  4.21 us
  transfers between devices with their start and end apart: 1, of which 0 were waited for; matrix products, arithmetic and copies ran while one was open for 14% of the time, Pallas kernels for 0%

commit v1 on v0

v1 whole, which is shorter than its diff:
```python
import jax
import jax.numpy as jnp
from jax import lax
from jax.sharding import Mesh
from jax.sharding import PartitionSpec as P

BLK = 128
OUT_SLOTS = 32
DP = ("dp_0", "dp_1", "dp_2")
DP_MP = ("dp_0", "dp_1", "dp_2", "mp")
LANES = 128

sharpness = 2.0


def routing(fill, target, target_slot, n_dp, n_mp, in_slots, own_dp, own_mp):
    col_shape = (n_dp, n_mp, in_slots)
    col_fill = lax.dynamic_index_in_dim(fill.reshape(col_shape), own_mp, 1, keepdims=False)
    col_target = lax.dynamic_index_in_dim(target.reshape(col_shape), own_mp, 1, keepdims=False)
    col_slot = lax.dynamic_index_in_dim(target_slot.reshape(col_shape), own_mp, 1, keepdims=False)
    own_target = lax.dynamic_index_in_dim(col_target, own_dp, 0, keepdims=False)
    own_fill = lax.dynamic_index_in_dim(col_fill, own_dp, 0, keepdims=False)
    goes = own_target[None, :] == jnp.arange(n_dp, dtype=jnp.int32)[:, None]
    slots = jnp.arange(in_slots, dtype=jnp.int32)[None, :]
    chosen = jnp.sum(jnp.where(goes, slots, 0), axis=1)
    lands = jnp.where(col_target == own_dp, col_slot, -1)
    places = jnp.arange(OUT_SLOTS, dtype=jnp.int32)[:, None, None]
    hits = lands[None] == places
    sources = jnp.arange(n_dp, dtype=jnp.int32)[None, :, None]
    gather_order = jnp.sum(jnp.where(hits, sources, 0), axis=(1, 2))
    out_fill = jnp.sum(jnp.where(hits, col_fill[None], 0), axis=(1, 2))
    return chosen, gather_order, out_fill, own_fill


def token_mask(fills):
    return (lax.broadcasted_iota(jnp.int32, (1, 1, BLK), 2) < fills[:, None, None]).astype(
        jnp.float32
    )


def local(latents, proj_weight, proj_bias, fill, target, target_slot):
    n_dp = lax.axis_size(DP)
    n_mp = lax.axis_size("mp")
    n_all = n_dp * n_mp
    own_dp = lax.axis_index(DP)
    own_mp = lax.axis_index("mp")
    feature_width = latents.shape[1]
    bits = proj_weight.shape[0]
    in_slots = latents.shape[0] // BLK
    chosen, gather_order, out_fill, own_fill = routing(
        fill, target, target_slot, n_dp, n_mp, in_slots, own_dp, own_mp
    )
    token_count = jnp.sum(fill).astype(jnp.float32)
    loaded = latents.reshape(in_slots, BLK, feature_width)
    dots = jnp.einsum("nkd,bd->nbk", loaded, proj_weight, preferred_element_type=jnp.float32)
    outgoing = dots.astype(jnp.float16)[chosen]
    scaled = sharpness * (dots + proj_bias[None, :, None])
    live = token_mask(own_fill)
    probability = jax.nn.sigmoid(scaled)
    entropy = jax.nn.softplus(scaled) - probability * scaled
    bit_sums = jnp.sum(probability * live, axis=(0, 2))
    entropy_sum = jnp.sum(entropy * live)
    variance = probability * (1.0 - probability) * live
    first_rounded = (-2.0 * scaled * variance).astype(jnp.bfloat16)
    second_rounded = (2.0 * variance).astype(jnp.bfloat16)
    first_weight = jnp.einsum(
        "nbk,nkd->db", first_rounded, loaded, preferred_element_type=jnp.float32
    )
    second_weight = jnp.einsum(
        "nbk,nkd->db", second_rounded, loaded, preferred_element_type=jnp.float32
    )
    common = jnp.concatenate([bit_sums, entropy_sum[None]])
    partial = jnp.concatenate(
        [
            first_weight,
            second_weight,
            jnp.broadcast_to(common[None], (feature_width, bits + 1)),
            jnp.zeros((feature_width, LANES - 3 * bits - 1), jnp.float32),
        ],
        axis=1,
    )
    width = feature_width // n_all
    partial = partial.reshape(n_all, width, LANES)
    partials = lax.all_to_all(partial, DP_MP, split_axis=0, concat_axis=0, tiled=True)
    arrived = lax.all_to_all(outgoing, DP, split_axis=0, concat_axis=0, tiled=True)
    sums = jnp.sum(partials, axis=0)
    marginal = sums[0, 2 * bits : 3 * bits] / token_count
    entropy_total = sums[0, 3 * bits]
    codebook = -jnp.sum(marginal * jnp.log(marginal) + (1.0 - marginal) * jnp.log(1.0 - marginal))
    entropy_loss = entropy_total / token_count - codebook
    log_odds = jnp.log(1.0 - marginal) - jnp.log(marginal)
    own_columns = (sums[:, :bits] - sums[:, bits : 2 * bits] * log_odds[None]) / jnp.sqrt(token_count)
    own_columns = jnp.pad(own_columns, ((0, 0), (0, LANES - bits)))
    columns = lax.all_to_all(
        jnp.broadcast_to(own_columns[None], (n_all, width, LANES)),
        DP_MP,
        split_axis=0,
        concat_axis=0,
        tiled=True,
    )
    weight_grad = columns.reshape(feature_width, LANES)[:, :bits].T
    landed = arrived[gather_order].astype(jnp.float32)
    scaled = sharpness * (landed + proj_bias[None, :, None])
    probability = jax.nn.sigmoid(scaled)
    variance = probability * (1.0 - probability) * token_mask(out_fill)
    cotangent = (-2.0 * scaled * variance - 2.0 * variance * log_odds[None, :, None]).astype(
        jnp.bfloat16
    )
    latent_grad = jnp.einsum(
        "nbk,bd->nkd", cotangent, proj_weight, preferred_element_type=jnp.float32
    ).astype(jnp.bfloat16)
    return (latent_grad.reshape(-1, feature_width), weight_grad, entropy_loss)


def solution(mesh):
    torus = Mesh(mesh.devices.reshape(8, 4, 2, mesh.shape["mp"]), DP_MP)
    in_specs = (P(DP_MP, None), P(), P(), P(), P(), P())
    out_specs = (P(DP_MP, None), P(), P())
    return jax.shard_map(local, mesh=torus, in_specs=in_specs, out_specs=out_specs, check_vma=False)
```

time: 118 us -> 83.3 us (0.71)
  blocking collectives: 72.6 us -> 0 us
  waiting for transfers between devices: 0.01 us -> 33.8 us
  starting transfers between devices: 9.05 us -> 26 us
  local copies, waits for them, and re-layouts: 19.7 us -> 6.44 us
    psum x4 -> x0, blocking collectives: 72.6 us -> none  [one_axis_at_a_time(): return functools.reduce(lax.psum, axes, x)]
    all_to_all x1 -> x3, waiting for transfers between devices: 0.01 us -> 33.8 us  [the longest x1 12.7 us: local(): lax.all_to_all(outgoing, DP, split_axis=0, concat_axis=0, tiled=True)]
    all_to_all x1 -> x3, starting transfers between devices: 9.05 us -> 26 us  [the longest x1 15.6 us: local(): lax.all_to_all(partial, DP_MP, split_axis=0, concat_axis=0, tiled=True)]
    scatter x2 -> x0, local copies, waits for them, and re-layouts: 16.3 us -> none  [the longest x1 15.5 us: routing(): jnp.zeros((OUT_SLOTS,), jnp.int32).at[landing]]
    concatenate x0 -> x2, other arithmetic: none -> 1.48 us  [the longest x1 0.77 us: local(): jnp.concatenate([first_weight, second_weight, jnp.broadcast_to(common[Non...]
  transfers between devices with their start and end apart: 1 -> 3, of which waited for: 0 -> 3; matrix products, arithmetic and copies ran while one was open for 14% -> 6% of each run, Pallas kernels for 0% -> 0%
where the time goes in v1:
time: 83.3 us; the launch traced here: 82.9 us
  waiting for transfers between devices  33.8 us (41%)
  starting transfers between devices  26 us (31%)
  matrix products  7.93 us (10%)
  local copies, waits for them, and re-layouts  6.44 us (8%)
  other arithmetic  4.84 us (6%)
  between operations  3.96 us (5%)
    all_to_all x1, starting transfers between devices, local(): lax.all_to_all(partial, DP_MP, split_axis=0, concat_axis=0, tiled=True)  15.6 us
    all_to_all x1, waiting for transfers between devices, local(): lax.all_to_all(outgoing, DP, split_axis=0, concat_axis=0, tiled=True)  12.7 us
    all_to_all x1, waiting for transfers between devices, local(): lax.all_to_all(jnp.broadcast_to(own_columns[None], (n_all, width, LANES))...  11.4 us
    all_to_all x1, waiting for transfers between devices, local(): lax.all_to_all(partial, DP_MP, split_axis=0, concat_axis=0, tiled=True)  9.72 us
    all_to_all x1, starting transfers between devices, local(): lax.all_to_all(jnp.broadcast_to(own_columns[None], (n_all, width, LANES))...  5.64 us
    all_to_all x1, starting transfers between devices, local(): lax.all_to_all(outgoing, DP, split_axis=0, concat_axis=0, tiled=True)  4.68 us
    dot_general x1, matrix products, local(): jnp.einsum('nkd,bd->nbk', loaded, proj_weight, preferred_element_type=jnp...  4.21 us
    dot_general x1, matrix products, local(): jnp.einsum('nbk,bd->nkd', cotangent, proj_weight, preferred_element_type=...  2.18 us
  transfers between devices with their start and end apart: 3, of which 3 were waited for; matrix products, arithmetic and copies ran while one was open for 6% of the time, Pallas kernels for 0%

profile of v1, /device:TPU:1, one launch (start us, length us, event | category | flops | bytes accessed | tf_op | source)
XLA Modules:
  0.0 82.9 jit_solution(15469074267978505357)
XLA Ops:
  0.6 0.0 copy-start
  0.7 0.9 %reshape.141 = s32[64,4,64]{2,1,0:T(4,128)S(1)} reshape(s32[16384]{0:T(1024)} %param.10) | data formatting | bytes 131072 | tf_op jit(solution)/shard_map/reshape | solution.py:19
  1.6 1.0 %reshape.143 = s32[64,4,64]{2,1,0:T(4,128)S(1)} reshape(s32[16384]{0:T(1024)} %param.9) | data formatting | bytes 131072 | tf_op jit(solution)/shard_map/reshape | solution.py:18
  2.6 0.1 fusion.27
  2.7 0.0 copy-done
  2.7 0.0 copy-start.3
  2.7 0.0 copy-start.4
  2.7 4.2 %multiply_reduce_fusion = (f32[18]{0:T(128)S(1)}, f32[]{:T(128)}, f32[18,64,128]{2,0,1:T(8,128)S(1)}) fusion(f32[64,128]{1,0:T(8,128)S(1)} %fusion.27, f32[18]{0:T(128)} %param.8, bf16[64,128,256]{2,1,0:T(8,128)(2,1)} %bitcast.105, bf16[18,256]{1,0:T(8,128)(2,1)S(1)} %copy-done), kind=kOutput, calls=%fused_computation.27 | convolution fusion | flops 78004208 | bytes 4826260 | tf_op jit(solution)/shard_map/nkd,bd->nbk/dot_general | solution.py:55
  6.9 0.0 copy-done.3
  6.9 0.0 copy-done.4
  6.9 0.8 convolution_bitcast_fusion
  7.7 0.0 copy-start.2
  7.7 0.0 copy-start.1
  7.7 0.8 convolution_bitcast_fusion.1
  8.5 0.1 copy.14
  8.6 0.1 copy.15
  8.7 0.1 pad.8.clone
  8.8 0.7 pad_maximum_fusion
  9.5 0.8 maximum_maximum_fusion
  10.3 15.6 %all-to-all-start.1 = ((f32[256,1,128]{2,1,0:T(1,128)}), f32[256,1,128]{2,1,0:T(1,128)S(1)}, u32[]{:S(2)}, u32[]{:S(2)}) async-start(f32[256,1,128]{2,1,0:T(1,128)} %bitcast.18), calls=%async_computation.1 | async-start | bytes 262144 | tf_op jit(solution)/shard_map/all_to_all | solution.py:84
  25.9 0.1 select_reduce_fusion.2
  26.1 0.0 copy-done.2
  26.1 0.1 reshape.142
  26.2 0.1 compare_select_fusion.1
  26.3 1.2 %select_reduce_fusion = (s32[32]{0:T(128)S(1)}, s32[32]{0:T(128)S(1)}) fusion(s32[64,64]{1,0:T(8,128)S(1)} %bitcast.101, s32[64,64]{1,0:T(8,128)S(1)} %bitcast.100), kind=kLoop, calls=%fused_computation.7 | loop fusion | flops 655296 | bytes 33024 | tf_op jit(solution)/shard_map/reduce_sum | solution.py:31
  27.5 0.0 copy-done.1
  27.5 0.7 reduce_sum.87
  28.9 0.1 convert_bitcast_fusion
  28.9 9.7 %all-to-all-done.1 = f32[256,1,128]{2,1,0:T(1,128)S(1)} async-done(((f32[256,1,128]{2,1,0:T(1,128)}), f32[256,1,128]{2,1,0:T(1,128)S(1)}, u32[]{:S(2)}, u32[]{:S(2)}) %all-to-all-start.1) | async-done | bytes 131104 | tf_op jit(solution)/shard_map/all_to_all | solution.py:84
  38.7 0.3 reduce_sum.85
  38.9 0.7 fusion.37
  39.6 0.1 subtract_divide_fusion
  39.7 0.7 broadcast_in_dim.86
  40.4 5.6 %all-to-all-start.2 = ((f32[256,1,128]{2,1,0:T(1,128)}), f32[256,1,128]{2,1,0:T(1,128)S(1)}, u32[]{:S(2)}, u32[]{:S(2)}) async-start(f32[256,1,128]{2,1,0:T(1,128)} %broadcast_in_dim.86), calls=%async_computation.2 | async-start | bytes 262144 | tf_op jit(solution)/shard_map/all_to_all | solution.py:94
  46.1 1.4 %gather_fusion = f16[64,18,128]{2,1,0:T(8,128)(2,1)} fusion(f16[64,18,128]{2,1,0:T(8,128)(2,1)S(1)} %convert_bitcast_fusion, s32[1024]{0:T(1024)S(1)} %pad_clamp_fusion.1), kind=kCustom, calls=%fused_computation | custom fusion | bytes 590080 | tf_op jit(solution)/shard_map/gather | solution.py:56
  47.5 0.1 fusion.28
  47.6 11.4 %all-to-all-done.2 = f32[256,1,128]{2,1,0:T(1,128)S(1)} async-done(((f32[256,1,128]{2,1,0:T(1,128)}), f32[256,1,128]{2,1,0:T(1,128)S(1)}, u32[]{:S(2)}, u32[]{:S(2)}) %all-to-all-start.2) | async-done | bytes 131104 | tf_op jit(solution)/shard_map/all_to_all | solution.py:94
  59.0 4.7 %all-to-all-start = ((f16[64,18,128]{2,1,0:T(8,128)(2,1)}), f16[64,18,128]{2,1,0:T(8,128)(2,1)S(1)}, u32[]{:S(2)}, u32[]{:S(2)}) async-start(f16[64,18,128]{2,1,0:T(8,128)(2,1)} %gather_fusion), calls=%async_computation | async-start | bytes 786432 | tf_op jit(solution)/shard_map/all_to_all | solution.py:85
  63.7 0.6 slice.19
  65.6 0.7 copy.16
  66.3 12.7 %all-to-all-done = f16[64,18,128]{2,1,0:T(8,128)(2,1)S(1)} async-done(((f16[64,18,128]{2,1,0:T(8,128)(2,1)}), f16[64,18,128]{2,1,0:T(8,128)(2,1)S(1)}, u32[]{:S(2)}, u32[]{:S(2)}) %all-to-all-start) | async-done | bytes 294944 | tf_op jit(solution)/shard_map/all_to_all | solution.py:85
  79.0 0.6 gather_fusion.1
  79.6 2.2 %convolution_convert_fusion = bf16[32,128,256]{2,1,0:T(8,128)(2,1)} fusion(f16[32,18,128]{2,1,0:T(8,128)(2,1)S(1)} %gather_fusion.1, f32[18]{0:T(128)S(1)} %fusion.38, f32[32,128]{1,0:T(8,128)S(1)} %fusion.28, f32[18]{0:T(128)S(1)} %copy-done.3, bf16[18,256]{1,0:T(8,128)(2,1)S(1)} %copy-done), kind=kOutput, calls=%fused_computation.3 | convolution fusion | flops 39829504 | bytes 2270352 | tf_op jit(solution)/shard_map/nbk,bd->nkd/dot_general | solution.py:109
  (9 shorter events, 0.1 us)
Async XLA Ops:
  0.6 2.0 %copy-start = (bf16[18,256]{1,0:T(8,128)(2,1)S(1)}, bf16[18,256]{1,0:T(8,128)(2,1)}, u32[]{:S(2)}) copy-start(bf16[18,256]{1,0:T(8,128)(2,1)} %param.7) | copy-start | bytes 27652
  2.7 4.2 %copy-start.3 = (f32[18]{0:T(128)S(1)}, f32[18]{0:T(128)}, u32[]{:S(2)}) copy-start(f32[18]{0:T(128)} %param.8) | copy-start | bytes 220
  2.7 4.2 %copy-start.4 = (bf16[8192,256]{1,0:T(8,128)(2,1)S(1)}, bf16[8192,256]{1,0:T(8,128)(2,1)}, u32[]{:S(2)}) copy-start(bf16[8192,256]{1,0:T(8,128)(2,1)} %param.6) | copy-start | bytes 12582916
  7.7 18.4 %copy-start.2 = (s32[16384]{0:T(1024)S(1)}, s32[16384]{0:T(1024)}, u32[]{:S(2)}) copy-start(s32[16384]{0:T(1024)} %param.11) | copy-start | bytes 196612
  7.7 19.8 %copy-start.1 = (s32[16384]{0:T(1024)S(1)}, s32[16384]{0:T(1024)}, u32[]{:S(2)}) copy-start(s32[16384]{0:T(1024)} %param.9) | copy-start | bytes 196612
  10.3 28.4 %all-to-all-start.1 = ((f32[256,1,128]{2,1,0:T(1,128)}), f32[256,1,128]{2,1,0:T(1,128)S(1)}, u32[]{:S(2)}, u32[]{:S(2)}) async-start(f32[256,1,128]{2,1,0:T(1,128)} %bitcast.18), calls=%async_computation.1 | async-start | bytes 262144 | tf_op jit(solution)/shard_map/all_to_all | solution.py:84
  40.4 18.6 %all-to-all-start.2 = ((f32[256,1,128]{2,1,0:T(1,128)}), f32[256,1,128]{2,1,0:T(1,128)S(1)}, u32[]{:S(2)}, u32[]{:S(2)}) async-start(f32[256,1,128]{2,1,0:T(1,128)} %broadcast_in_dim.86), calls=%async_computation.2 | async-start | bytes 262144 | tf_op jit(solution)/shard_map/all_to_all | solution.py:94
  59.0 20.0 %all-to-all-start = ((f16[64,18,128]{2,1,0:T(8,128)(2,1)}), f16[64,18,128]{2,1,0:T(8,128)(2,1)S(1)}, u32[]{:S(2)}, u32[]{:S(2)}) async-start(f16[64,18,128]{2,1,0:T(8,128)(2,1)} %gather_fusion), calls=%async_computation | async-start | bytes 786432 | tf_op jit(solution)/shard_map/all_to_all | solution.py:85

commit v2 on v1

v2 whole, which is shorter than its diff:
```python
import jax
import jax.numpy as jnp
from jax import lax
from jax.sharding import Mesh
from jax.sharding import PartitionSpec as P

BLK = 128
LANES = 128
OUT_SLOTS = 32
DP = ("dp_0", "dp_1", "dp_2")
DP_MP = ("dp_0", "dp_1", "dp_2", "mp")
FINE = 2048.0
ENTROPY_UNIT = 8.0

sharpness = 2.0


def logistic(scaled):
    decay = jnp.exp(-jnp.abs(scaled))
    inverse = 1.0 / (1.0 + decay)
    return decay, inverse, decay * inverse


def token_mask(fills):
    return lax.broadcasted_iota(jnp.int32, (1, 1, BLK), 2) < fills[:, None, None]


def statistics(dots, loaded, proj_bias, own_fill):
    scaled = sharpness * (dots + proj_bias[None, :, None])
    live = token_mask(own_fill)
    decay, inverse, tail = logistic(scaled)
    probability = jnp.where(scaled >= 0.0, inverse, tail)
    entropy = jnp.log1p(decay) + jnp.abs(scaled) * tail
    bit_sums = jnp.sum(jnp.where(live, probability, 0.0), axis=(0, 2))
    entropy_sum = jnp.sum(jnp.where(live, entropy, 0.0))
    second = jnp.where(live, 2.0 * (tail * inverse), 0.0)
    first_weight = jnp.einsum(
        "nbk,nkd->db",
        (-scaled * second).astype(jnp.bfloat16),
        loaded,
        preferred_element_type=jnp.float32,
    )
    second_weight = jnp.einsum(
        "nbk,nkd->db", second.astype(jnp.bfloat16), loaded, preferred_element_type=jnp.float32
    )
    return bit_sums, entropy_sum, first_weight, second_weight


def two_halves(values):
    coarse = values.astype(jnp.float16)
    fine = ((values - coarse.astype(jnp.float32)) * FINE).astype(jnp.float16)
    return coarse, fine


def over_mp(values):
    values = values + lax.ppermute(values, "mp", [(0, 1), (1, 0), (2, 3), (3, 2)])
    return values + lax.ppermute(values, "mp", [(0, 3), (3, 0), (1, 2), (2, 1)])


def landing(fill, target, target_slot, n_dp, in_slots, own_dp, own_mp):
    def column(values):
        return lax.dynamic_slice_in_dim(values.reshape(n_dp, -1), own_mp * in_slots, in_slots, 1)

    col_fill, col_target, col_slot = column(fill), column(target), column(target_slot)
    lands = jnp.where(col_target == own_dp, col_slot, -1)
    places = jnp.arange(OUT_SLOTS, dtype=jnp.int32)[:, None, None]
    hits = lands[None] == places
    sources = jnp.arange(n_dp, dtype=jnp.int32)[None, :, None]
    gather_order = jnp.sum(jnp.where(hits, sources, 0), axis=(1, 2))
    out_fill = jnp.sum(jnp.where(hits, col_fill[None], 0), axis=(1, 2))
    return gather_order, out_fill


def local(latents, proj_weight, proj_bias, fill, target, target_slot):
    n_dp = lax.axis_size(DP)
    n_mp = lax.axis_size("mp")
    own_dp = lax.axis_index(DP)
    own_mp = lax.axis_index("mp")
    width = latents.shape[1]
    bits = proj_weight.shape[0]
    in_slots = latents.shape[0] // BLK
    parts = width // n_dp
    own_start = (own_dp * n_mp + own_mp) * in_slots
    own_target = lax.dynamic_slice_in_dim(target, own_start, in_slots)
    own_fill = lax.dynamic_slice_in_dim(fill, own_start, in_slots)
    goes = own_target[None, :] == jnp.arange(n_dp, dtype=jnp.int32)[:, None]
    chosen = jnp.sum(jnp.where(goes, jnp.arange(in_slots, dtype=jnp.int32)[None, :], 0), axis=1)
    loaded = latents.reshape(in_slots, BLK, width)
    dots = jnp.einsum("nkd,bd->nbk", loaded, proj_weight, preferred_element_type=jnp.float32)
    bit_sums, entropy_sum, first_weight, second_weight = statistics(
        dots, loaded, proj_bias, own_fill
    )
    common = jnp.concatenate([bit_sums, entropy_sum[None] / ENTROPY_UNIT])
    common = jnp.broadcast_to(common[None], (width, bits + 1))
    partial = jnp.concatenate([first_weight, second_weight, common], axis=1)
    coarse, fine = two_halves(partial)
    used = 3 * bits + 1
    coarse = jnp.pad(coarse, ((0, 0), (0, LANES // 2 - used)))
    fine = jnp.pad(fine, ((0, 0), (0, LANES // 2 - used)))
    partial = jnp.concatenate([coarse, fine], axis=1)
    partial = jnp.transpose(partial.reshape(parts, n_dp, LANES), (1, 0, 2))
    outgoing = jnp.concatenate([dots.astype(jnp.float16)[chosen], partial], axis=1)
    arrived = lax.all_to_all(outgoing, DP, split_axis=0, concat_axis=0, tiled=True)
    token_count = jnp.sum(fill).astype(jnp.float32)
    gather_order, out_fill = landing(fill, target, target_slot, n_dp, in_slots, own_dp, own_mp)
    sums = jnp.sum(arrived[:, bits:].astype(jnp.float32), axis=0)
    sums = sums[:, : LANES // 2] + sums[:, LANES // 2 :] / FINE
    sums = over_mp(sums)
    totals = sums[0]
    marginal = totals[2 * bits : 3 * bits] / token_count
    log_odds = jnp.log(1.0 - marginal) - jnp.log(marginal)
    codebook = -jnp.sum(marginal * jnp.log(marginal) + (1.0 - marginal) * jnp.log(1.0 - marginal))
    entropy_loss = totals[3 * bits] * ENTROPY_UNIT / token_count - codebook
    columns = sums[:, :bits] - sums[:, bits : 2 * bits] * log_odds[None]
    columns = (columns / jnp.sqrt(token_count)).reshape(1, parts * bits)
    columns = jnp.pad(columns, ((0, 0), (0, LANES - parts * bits)))
    columns = lax.all_to_all(
        jnp.broadcast_to(columns[None], (n_dp, 1, LANES)), DP, split_axis=0, concat_axis=0, tiled=True
    )
    columns = columns.reshape(n_dp, LANES)[:, : parts * bits].T.reshape(parts, bits, n_dp)
    weight_grad = jnp.transpose(columns, (1, 0, 2)).reshape(bits, width)
    landed = arrived[gather_order][:, :bits].astype(jnp.float32)
    scaled = sharpness * (landed + proj_bias[None, :, None])
    _, inverse, tail = logistic(scaled)
    second = jnp.where(token_mask(out_fill), 2.0 * (tail * inverse), 0.0)
    cotangent = (-second * (scaled + log_odds[None, :, None])).astype(jnp.bfloat16)
    latent_grad = jnp.einsum(
        "nbk,bd->nkd", cotangent, proj_weight, preferred_element_type=jnp.float32
    ).astype(jnp.bfloat16)
    return (latent_grad.reshape(-1, width), weight_grad, entropy_loss)


def solution(mesh):
    torus = Mesh(mesh.devices.reshape(8, 4, 2, mesh.shape["mp"]), DP_MP)
    in_specs = (P(DP_MP, None), P(), P(), P(), P(), P())
    out_specs = (P(DP_MP, None), P(), P())
    return jax.shard_map(local, mesh=torus, in_specs=in_specs, out_specs=out_specs, check_vma=False)
```

time: 83.3 us -> 66.2 us (0.79)
  waiting for transfers between devices: 33.8 us -> 20.2 us
  starting transfers between devices: 26 us -> 23.8 us
  local copies, waits for them, and re-layouts: 6.44 us -> 4.74 us
    all_to_all x2 -> x1, waiting for transfers between devices: 21.1 us -> 5.3 us  [local(): lax.all_to_all(jnp.broadcast_to(columns[None], (n_dp, 1, LANES)), DP, spl...]
    all_to_all x2 -> x1, starting transfers between devices: 21.3 us -> 6.91 us  [local(): lax.all_to_all(jnp.broadcast_to(columns[None], (n_dp, 1, LANES)), DP, spl...]
    all_to_all x1, starting transfers between devices: 4.68 us -> 13.1 us  [local(): lax.all_to_all(outgoing, DP, split_axis=0, concat_axis=0, tiled=True)]
    ppermute x0 -> x2, starting transfers between devices: none -> 3.71 us  [the longest x1 2.48 us: over_mp(): return values + lax.ppermute(values, 'mp', [(0, 3), (3, 0), (1, 2), (2, 1)])]
    ppermute x0 -> x2, waiting for transfers between devices: none -> 1.22 us  [the longest x1 1.22 us: over_mp(): lax.ppermute(values, 'mp', [(0, 1), (1, 0), (2, 3), (3, 2)])]
    reshape x3 -> x7, local copies, waits for them, and re-layouts: 2.01 us -> 0.91 us  [the longest x1 0.7 us: local(): weight_grad = jnp.transpose(columns, (1, 0, 2)).reshape(bits, width)]
    dynamic_slice x0 -> x2, local copies, waits for them, and re-layouts: none -> 1 us  [the longest x1 0.92 us: local(): own_fill = lax.dynamic_slice_in_dim(fill, own_start, in_slots)]
    all_to_all x1, waiting for transfers between devices: 12.7 us -> 13.6 us  [local(): lax.all_to_all(outgoing, DP, split_axis=0, concat_axis=0, tiled=True)]
  transfers between devices with their start and end apart: 3 -> 4, of which waited for: 3 -> 3; matrix products, arithmetic and copies ran while one was open for 6% -> 8% of each run, Pallas kernels for 0% -> 0%
where the time goes in v2:
time: 66.2 us; the launch traced here: 65.9 us
  starting transfers between devices  23.8 us (36%)
  waiting for transfers between devices  20.2 us (31%)
  matrix products  8.11 us (12%)
  local copies, waits for them, and re-layouts  4.74 us (7%)
  between operations  4.69 us (7%)
  other arithmetic  4.4 us (7%)
    all_to_all x1, waiting for transfers between devices, local(): lax.all_to_all(outgoing, DP, split_axis=0, concat_axis=0, tiled=True)  13.6 us
    all_to_all x1, starting transfers between devices, local(): lax.all_to_all(outgoing, DP, split_axis=0, concat_axis=0, tiled=True)  13.1 us
    all_to_all x1, starting transfers between devices, local(): lax.all_to_all(jnp.broadcast_to(columns[None], (n_dp, 1, LANES)), DP, spl...  6.91 us
    all_to_all x1, waiting for transfers between devices, local(): lax.all_to_all(jnp.broadcast_to(columns[None], (n_dp, 1, LANES)), DP, spl...  5.3 us
    dot_general x1, matrix products, local(): jnp.einsum('nkd,bd->nbk', loaded, proj_weight, preferred_element_type=jnp...  4.31 us
    ppermute x1, starting transfers between devices, over_mp(): return values + lax.ppermute(values, 'mp', [(0, 3), (3, 0), (1, 2), (2, 1)])  2.48 us
    dot_general x1, matrix products, local(): jnp.einsum('nbk,bd->nkd', cotangent, proj_weight, preferred_element_type=...  2.18 us
  transfers between devices with their start and end apart: 4, of which 3 were waited for; matrix products, arithmetic and copies ran while one was open for 8% of the time, Pallas kernels for 0%

profile of v2, /device:TPU:1, one launch (start us, length us, event | category | flops | bytes accessed | tf_op | source)
XLA Modules:
  0.0 65.9 jit_solution(2033103956212599712)
XLA Ops:
  0.6 0.0 copy-start
  0.7 0.0 copy-start.5
  0.7 0.0 copy-start.4
  0.7 0.9 %dynamic_slice.19 = s32[64]{0:T(128)S(1)} dynamic-slice(s32[16384]{0:T(1024)} %param.9, s32[]{:T(128)S(6)} %select_n.66), dynamic_slice_sizes={64} | dynamic-slice | bytes 516 | tf_op jit(solution)/shard_map/dynamic_slice | solution.py:85
  1.6 0.1 iota_compare_fusion.3
  1.7 0.0 copy-done
  1.7 4.3 %select_reduce_fusion.2 = (f32[18]{0:T(128)S(1)}, f32[]{:T(128)}, f32[18,64,128]{2,0,1:T(8,128)S(1)}) fusion(f32[18]{0:T(128)} %param.8, pred[64,128]{1,0:T(8,128)(4,1)S(1)} %iota_compare_fusion.3, bf16[64,128,256]{2,1,0:T(8,128)(2,1)} %bitcast.100, bf16[18,256]{1,0:T(8,128)(2,1)S(1)} %copy-done), kind=kOutput, calls=%fused_computation.16 | convolution fusion | flops 77709296 | bytes 4801684 | tf_op jit(solution)/shard_map/nkd,bd->nbk/dot_general | solution.py:89
  6.0 0.0 copy-done.5
  6.0 0.0 copy-done.4
  6.0 0.8 %convolution_bitcast_fusion = f32[256,18]{0,1:T(8,128)S(1)} fusion(bf16[64,128,256]{2,1,0:T(8,128)(2,1)S(1)} %bitcast.101, f32[18,64,128]{2,0,1:T(8,128)S(1)} %get-tuple-element.11, f32[18]{0:T(128)S(1)} %copy-done.5, pred[64,128]{1,0:T(8,128)(4,1)S(1)} %iota_compare_fusion.3), kind=kOutput, calls=%fused_computation.3 | convolution fusion | flops 77119488 | bytes 4810824 | tf_op jit(solution)/shard_map/nbk,nkd->db/dot_general | solution.py:43
  6.8 0.0 copy-start.2
  6.8 0.0 copy-start.1
  6.8 0.0 copy-start.3
  6.8 0.8 %convolution_bitcast_fusion.1 = f32[256,18]{0,1:T(8,128)S(1)} fusion(bf16[64,128,256]{2,1,0:T(8,128)(2,1)S(1)} %bitcast.102, f32[18,64,128]{2,0,1:T(8,128)S(1)} %get-tuple-element.11, f32[18]{0:T(128)S(1)} %copy-done.5, pred[64,128]{1,0:T(8,128)(4,1)S(1)} %iota_compare_fusion.3), kind=kOutput, calls=%fused_computation.4 | convolution fusion | flops 77414400 | bytes 4810824 | tf_op jit(solution)/shard_map/nbk,nkd->db/dot_general | solution.py:37
  7.7 0.1 convert_bitcast_fusion
  8.4 0.1 pad_maximum_fusion.1
  8.4 0.1 fusion.26
  8.6 0.1 copy.28
  8.7 0.1 copy.33
  8.8 0.0 copy-done.2
  8.8 0.1 dynamic_slice.18
  8.9 0.1 select_reduce_fusion.3
  9.0 0.7 %gather_fusion = f16[64,18,128]{2,1,0:T(8,128)(2,1)S(1)} fusion(f16[64,18,128]{2,1,0:T(8,128)(2,1)S(1)} %convert_bitcast_fusion, s32[1024]{0:T(1024)S(1)} %pad_clamp_fusion.1), kind=kCustom, calls=%fused_computation | custom fusion | bytes 590080 | tf_op jit(solution)/shard_map/gather | solution.py:102
  9.7 0.9 %pad_maximum_fusion = f16[64,22,128]{2,1,0:T(8,128)(2,1)} fusion(f16[64,4,128]{2,1,0:T(4,128)(2,1)S(1)} %bitcast.97, f16[64,18,128]{2,1,0:T(8,128)(2,1)S(1)} %gather_fusion), kind=kLoop, calls=%fused_computation.27 | loop fusion | flops 180224 | bytes 720896 | tf_op jit(solution)/shard_map/concatenate | solution.py:102
  10.6 13.1 %all-to-all-start = ((f16[64,22,128]{2,1,0:T(8,128)(2,1)}), f16[64,22,128]{2,1,0:T(8,128)(2,1)S(1)}, u32[]{:S(2)}, u32[]{:S(2)}) async-start(f16[64,22,128]{2,1,0:T(8,128)(2,1)} %pad_maximum_fusion), calls=%async_computation | async-start | bytes 786432 | tf_op jit(solution)/shard_map/all_to_all | solution.py:103
  23.8 0.0 copy-done.1
  23.8 0.0 copy-done.3
  23.9 0.1 dynamic-slice_select_fusion
  24.0 1.2 %select_reduce_fusion.1 = (s32[32]{0:T(128)S(1)}, s32[32]{0:T(128)S(1)}) fusion(s32[64,64]{1,0:T(8,128)S(1)} %get-tuple-element.13, s32[64,64]{1,0:T(8,128)S(1)} %get-tuple-element.12), kind=kLoop, calls=%fused_computation.6 | loop fusion | flops 655296 | bytes 33024 | tf_op jit(solution)/shard_map/reduce_sum | solution.py:70
  25.2 0.1 iota_compare_fusion.5
  25.3 13.6 %all-to-all-done = f16[64,22,128]{2,1,0:T(8,128)(2,1)S(1)} async-done(((f16[64,22,128]{2,1,0:T(8,128)(2,1)}), f16[64,22,128]{2,1,0:T(8,128)(2,1)S(1)}, u32[]{:S(2)}, u32[]{:S(2)}) %all-to-all-start) | async-done | bytes 360480 | tf_op jit(solution)/shard_map/all_to_all | solution.py:103
  38.9 0.1 convert_reduce_fusion
  39.0 0.1 multiply_add_fusion
  39.1 1.2 %collective-permute-start = (f32[4,64]{1,0:T(4,128)S(1)}, f32[4,64]{1,0:T(4,128)S(1)}, u32[]{:S(2)}, u32[]{:S(2)}) collective-permute-start(f32[4,64]{1,0:T(4,128)S(1)} %multiply_add_fusion), channel_id=1, source_target_pairs={{0,1},{1,0},{2,3},{3,2},{4,5},{5,4},{6,7},{7,6},{8,9},{9,8},{10,11... | collective-permute-start | bytes 3080 | tf_op jit(solution)/shard_map/ppermute | solution.py:56
  40.3 1.2 %collective-permute-done = f32[4,64]{1,0:T(4,128)S(1)} collective-permute-done((f32[4,64]{1,0:T(4,128)S(1)}, f32[4,64]{1,0:T(4,128)S(1)}, u32[]{:S(2)}, u32[]{:S(2)}) %collective-permute-start) | collective-permute-done | bytes 1056 | tf_op jit(solution)/shard_map/ppermute | solution.py:56
  41.5 0.1 fusion.41
  41.6 2.5 %collective-permute-start.1 = (f32[4,64]{1,0:T(4,128)S(1)}, f32[4,64]{1,0:T(4,128)S(1)}, u32[]{:S(2)}, u32[]{:S(2)}) collective-permute-start(f32[4,64]{1,0:T(4,128)S(1)} %fusion.41), channel_id=1, source_target_pairs={{0,3},{3,0},{1,2},{2,1},{4,7},{7,4},{5,6},{6,5},{8,11},{11,8},{9,1... | collective-permute-start | bytes 3080 | tf_op jit(solution)/shard_map/ppermute | solution.py:57
  44.1 0.6 reduce_sum.84
  45.4 0.6 gather_fusion.1
  46.1 0.0 collective-permute-done.1
  46.1 0.7 %fusion.33 = (f32[]{:T(128)}, f32[1,18]{1,0:T(1,128)S(1)}) fusion(f32[]{:T(128)S(6)} %convert_element_type.50, f32[4,64]{1,0:T(4,128)S(1)} %add.114), kind=kLoop, calls=%fused_computation.74 | loop fusion | flops 107 | bytes 152 | tf_op jit(solution)/shard_map/reduce_sum | solution.py:112
  46.8 0.1 subtract_divide_fusion
  46.9 0.1 reshape.136
  47.0 0.6 broadcast_in_dim.115
  47.6 6.9 %all-to-all-start.1 = ((f32[64,1,128]{2,1,0:T(1,128)}), f32[64,1,128]{2,1,0:T(1,128)S(1)}, u32[]{:S(2)}, u32[]{:S(2)}) async-start(f32[64,1,128]{2,1,0:T(1,128)} %broadcast_in_dim.115), calls=%async_computation.1 | async-start | bytes 65536 | tf_op jit(solution)/shard_map/all_to_all | solution.py:117
  54.5 2.2 %convolution_convert_fusion = bf16[32,128,256]{2,1,0:T(8,128)(2,1)} fusion(f16[32,22,128]{2,1,0:T(8,128)(2,1)S(1)} %gather_fusion.1, f32[18]{0:T(128)S(1)} %log_subtract_fusion, f32[18]{0:T(128)S(1)} %copy-done.5, pred[32,128]{1,0:T(8,128)(4,1)S(1)} %iota_compare_fusion.5, bf16[18,256]{1,0:T(8,128)(2,1)S(1)} %copy-done), kind=kOutput, calls=%fused_computation.2 | convolution fusion | flops 39903232 | bytes 2290832 | tf_op jit(solution)/shard_map/nbk,bd->nkd/dot_general | solution.py:127
  56.7 0.6 slice.40
  58.6 5.3 %all-to-all-done.1 = f32[64,1,128]{2,1,0:T(1,128)S(1)} async-done(((f32[64,1,128]{2,1,0:T(1,128)}), f32[64,1,128]{2,1,0:T(1,128)S(1)}, u32[]{:S(2)}, u32[]{:S(2)}) %all-to-all-start.1) | async-done | bytes 32800 | tf_op jit(solution)/shard_map/all_to_all | solution.py:117
  63.9 0.1 copy.30
  64.0 0.7 %reshape.139 = f32[18,256]{1,0:T(8,128)} reshape(f32[18,4,64]{2,1,0:T(4,128)S(1)} %copy.31) | data formatting | bytes 36864 | tf_op jit(solution)/shard_map/reshape | solution.py:121
  (15 shorter events, 0.1 us)
Async XLA Ops:
  0.6 1.0 %copy-start = (bf16[18,256]{1,0:T(8,128)(2,1)S(1)}, bf16[18,256]{1,0:T(8,128)(2,1)}, u32[]{:S(2)}) copy-start(bf16[18,256]{1,0:T(8,128)(2,1)} %param.7) | copy-start | bytes 27652
  0.7 5.3 %copy-start.5 = (f32[18]{0:T(128)S(1)}, f32[18]{0:T(128)}, u32[]{:S(2)}) copy-start(f32[18]{0:T(128)} %param.8) | copy-start | bytes 220
  0.7 5.3 %copy-start.4 = (bf16[8192,256]{1,0:T(8,128)(2,1)S(1)}, bf16[8192,256]{1,0:T(8,128)(2,1)}, u32[]{:S(2)}) copy-start(bf16[8192,256]{1,0:T(8,128)(2,1)} %param.6) | copy-start | bytes 12582916
  6.8 2.0 %copy-start.2 = (s32[16384]{0:T(1024)S(1)}, s32[16384]{0:T(1024)}, u32[]{:S(2)}) copy-start(s32[16384]{0:T(1024)} %param.10) | copy-start | bytes 196612
  6.8 17.0 %copy-start.1 = (s32[16384]{0:T(1024)S(1)}, s32[16384]{0:T(1024)}, u32[]{:S(2)}) copy-start(s32[16384]{0:T(1024)} %param.9) | copy-start | bytes 196612
  6.8 17.0 %copy-start.3 = (s32[16384]{0:T(1024)S(1)}, s32[16384]{0:T(1024)}, u32[]{:S(2)}) copy-start(s32[16384]{0:T(1024)} %param.11) | copy-start | bytes 196612
  10.6 28.3 %all-to-all-start = ((f16[64,22,128]{2,1,0:T(8,128)(2,1)}), f16[64,22,128]{2,1,0:T(8,128)(2,1)S(1)}, u32[]{:S(2)}, u32[]{:S(2)}) async-start(f16[64,22,128]{2,1,0:T(8,128)(2,1)} %pad_maximum_fusion), calls=%async_computation | async-start | bytes 786432 | tf_op jit(solution)/shard_map/all_to_all | solution.py:103
  39.1 2.5 %collective-permute-start = (f32[4,64]{1,0:T(4,128)S(1)}, f32[4,64]{1,0:T(4,128)S(1)}, u32[]{:S(2)}, u32[]{:S(2)}) collective-permute-start(f32[4,64]{1,0:T(4,128)S(1)} %multiply_add_fusion), channel_id=1, source_target_pairs={{0,1},{1,0},{2,3},{3,2},{4,5},{5,4},{6,7},{7,6},{8,9},{9,8},{10,11... | collective-permute-start | bytes 3080 | tf_op jit(solution)/shard_map/ppermute | solution.py:56
  41.6 4.5 %collective-permute-start.1 = (f32[4,64]{1,0:T(4,128)S(1)}, f32[4,64]{1,0:T(4,128)S(1)}, u32[]{:S(2)}, u32[]{:S(2)}) collective-permute-start(f32[4,64]{1,0:T(4,128)S(1)} %fusion.41), channel_id=1, source_target_pairs={{0,3},{3,0},{1,2},{2,1},{4,7},{7,4},{5,6},{6,5},{8,11},{11,8},{9,1... | collective-permute-start | bytes 3080 | tf_op jit(solution)/shard_map/ppermute | solution.py:57
  47.6 16.3 %all-to-all-start.1 = ((f32[64,1,128]{2,1,0:T(1,128)}), f32[64,1,128]{2,1,0:T(1,128)S(1)}, u32[]{:S(2)}, u32[]{:S(2)}) async-start(f32[64,1,128]{2,1,0:T(1,128)} %broadcast_in_dim.115), calls=%async_computation.1 | async-start | bytes 65536 | tf_op jit(solution)/shard_map/all_to_all | solution.py:117
